TPU v7x, 32 devices: a whole 2x2x4 slice. The times are simulated.
32 devices in a mesh: samp: 8 (over y, x, core), par: 4 (over z).
Axes of the slice: x: 2, y: 2, z: 4, core: 2. Of those that a mesh axis runs over, the one named last changes fastest.
Arguments:
- log_derivs: bfloat16 [512, 262144], P('samp', 'par')
- energies: float32 [512, 8], P('samp'), may hold values from -6 to 6
- nys_rows: int32 [8, 8], P('samp'), may hold values from 0 to 63, as said below
Outputs:
- update: float32 [262144, 8], P('par')
- solution: float32 [512, 8], P('samp')
Inputs may be any that keep to these rules, and one draw needn't show every extreme that they name: `nys_rows`: each row holds 8 different local sample numbers of that group.
All inputs are finite; a program needn't handle non-finite values.
Results may differ from a plain program's by a relative error of at most 0.014.
Values may be sent and summed in bfloat16 or wider, within the bound.
A program may use at most 128 MiB of HBM per device.

v0:
```python
import math
import jax
import jax.numpy as jnp
from jax import lax
from jax.sharding import PartitionSpec as P

ITERS = 2
damping = 0.5


def factor_solve(factor, right):
    middle = lax.linalg.triangular_solve(factor, right, left_side=True, lower=True)
    return lax.linalg.triangular_solve(factor, middle, left_side=True, lower=True, transpose_a=True)


def small_solve(matrix, right):
    return factor_solve(jnp.linalg.cholesky(matrix), right)


def hdot(left, right):
    return jnp.dot(left, right, precision=lax.Precision.HIGHEST)


def gram_body(log_derivs, energies, nys_rows):
    samp_rows = log_derivs.shape[0]
    groups = lax.axis_size("samp")
    total_rows = samp_rows * groups
    total_cols = log_derivs.shape[1] * lax.axis_size("par")
    slab = lax.all_to_all(log_derivs, "samp", split_axis=1, concat_axis=0, tiled=True)
    widened = slab.astype(jnp.float32)
    col_mean = jnp.sum(widened, axis=0) / total_rows
    centered = ((widened - col_mean) * (1.0 / math.sqrt(total_cols))).astype(jnp.bfloat16)
    gram = lax.psum(
        jnp.einsum("rc,kc->rk", centered, centered, preferred_element_type=jnp.float32),
        ("samp", "par"),
    )
    all_energies = lax.all_gather(energies, "samp", axis=0, tiled=True)
    all_picks = lax.all_gather(nys_rows, "samp", axis=0, tiled=True)
    selected = (jnp.arange(groups, dtype=jnp.int32)[:, None] * samp_rows + all_picks).reshape(-1)
    sketch = jnp.take(gram, selected, axis=1)
    core_block = jnp.take(sketch, selected, axis=0)
    factor = jnp.linalg.cholesky(damping * core_block + hdot(sketch.T, sketch))

    def precondition(residual):
        coeffs = factor_solve(factor, hdot(sketch.T, residual))
        result = (residual - hdot(sketch, coeffs)) / damping
        return (result, hdot(result.T, residual))

    solution = jnp.zeros(all_energies.shape, jnp.float32)
    residual = all_energies
    precond_res, inner_prev = precondition(residual)
    direction = precond_res
    for iteration in range(ITERS):
        rounded = direction.astype(jnp.bfloat16).astype(jnp.float32)
        image_k = hdot(gram, rounded) + damping * direction
        curvature = hdot(direction.T, image_k)
        alpha_k = small_solve(curvature, inner_prev)
        solution = solution + hdot(direction, alpha_k)
        if iteration + 1 < ITERS:
            residual = residual - hdot(image_k, alpha_k)
            precond_res, inner_next = precondition(residual)
            beta_k = small_solve(inner_prev, inner_next)
            direction = precond_res + hdot(direction, beta_k)
            inner_prev = inner_next
    rounded_sol = solution.astype(jnp.bfloat16)
    local_update = jnp.einsum(
        "rc,rv->cv", centered, rounded_sol, preferred_element_type=jnp.float32
    )
    update = lax.all_gather(local_update.astype(jnp.bfloat16), "samp", axis=0, tiled=True).astype(
        local_update.dtype
    )
    start = lax.axis_index("samp") * samp_rows
    return (update, lax.dynamic_slice_in_dim(solution, start, samp_rows, 0))


def body(log_derivs, energies, nys_rows):
    update, solution = gram_body(log_derivs, energies, nys_rows)
    return (update, solution)


def solution(mesh):
    return jax.shard_map(
        body,
        mesh=mesh,
        in_specs=(P("samp", "par"), P("samp", None), P("samp", None)),
        out_specs=(P("par", None), P("samp", None)),
        check_vma=False,
    )
```

profile of v0, /device:TPU:0, one launch (start us, length us, event | category | flops | bytes accessed | tf_op | source)
XLA Modules:
  0.0 351.4 jit_solution(1456690422608163181)
XLA Ops:
  7.2 7.6 %copy.62 = bf16[8,8,8,8192]{3,2,0,1:T(8,128)(2,1)} copy(bf16[8,8,8,8192]{3,2,1,0:T(8,128)(2,1)} %bitcast.122) | data formatting | bytes 16777216 | tf_op jit(solution)/shard_map/all_to_all | solution.py:29
  14.8 5.3 %all-to-all-start = ((bf16[64,8,8192]{2,0,1:T(8,128)(2,1)}), bf16[64,8,8192]{2,0,1:T(8,128)(2,1)}, u32[]{:S(2)}, u32[]{:S(2)}) async-start(bf16[64,8,8192]{2,0,1:T(8,128)(2,1)} %bitcast.121), calls=%async_computation | async-start | bytes 16777216 | tf_op jit(solution)/shard_map/all_to_all | solution.py:29
  20.1 97.4 %all-gather.1 = s32[8,1,8]{2,1,0:T(1,128)S(1)} all-gather(s32[1,1,8]{2,1,0:T(1,128)S(1)} %bitcast.126), channel_id=1, replica_groups=mesh['samp'=8,'par'=4] {'samp'}, dimensions={0}, use_global_device_ids=true | all-gather | bytes 288 | tf_op jit(solution)/shard_map/all_gather | solution.py:38
  117.7 8.3 %all-gather = f32[8,64,8]{1,2,0:T(8,128)S(1)} all-gather(f32[1,64,8]{1,2,0:T(8,128)S(1)} %bitcast.125), channel_id=1, replica_groups=mesh['samp'=8,'par'=4] {'samp'}, dimensions={0}, use_global_device_ids=true | all-gather | bytes 18432 | tf_op jit(solution)/shard_map/all_gather | solution.py:37
  126.1 5.5 %convert_reduce_fusion = f32[8192]{0:T(1024)S(1)} fusion(bf16[64,8,8192]{2,0,1:T(8,128)(2,1)} %all-to-all-done), kind=kLoop, calls=%fused_computation.8 | loop fusion | flops 8380416 | bytes 8421376 | tf_op jit(solution)/shard_map/reduce_sum | solution.py:31
  131.6 8.9 %multiply_convert_fusion = bf16[64,8,8192]{2,0,1:T(8,128)(2,1)} fusion(bf16[64,8,8192]{2,0,1:T(8,128)(2,1)} %all-to-all-done, f32[8192]{0:T(1024)S(1)} %broadcast_multiply_fusion), kind=kLoop, calls=%fused_computation.5 | loop fusion | flops 16777216 | bytes 16809984 | tf_op jit(solution)/shard_map/convert.2
  140.5 11.3 %fusion.73 = f32[512,512]{1,0:T(8,128)} fusion(bf16[512,8192]{1,0:T(8,128)(2,1)} %bitcast.123), kind=kOutput, calls=%fused_computation.118 | convolution fusion | flops 4294967296 | bytes 9437184 | tf_op jit(solution)/shard_map/rc,kc->rk/dot_general | solution.py:34
  152.0 8.9 %fusion.1 = bf16[512,8192]{1,0:T(8,128)(2,1)} fusion(bf16[64,8,8192]{2,0,1:T(8,128)(2,1)} %all-to-all-done, f32[8192]{0:T(1024)S(1)} %broadcast_multiply_fusion), kind=kLoop, calls=%fused_computation.4 | loop fusion | flops 16777216 | bytes 16809984 | tf_op jit(solution)/shard_map/convert_element_type | solution.py:32
  160.9 122.7 %all-reduce.2.cloned.1.call-done = f32[512,512]{1,0:T(8,128)} async-done(((f32[512,512]{1,0:T(8,128)}), f32[512,512]{1,0:T(8,128)}) %all-reduce.2.cloned.1.call-update) | async-done | bytes 1048592 | tf_op jit(solution)/shard_map/psum | solution.py:33
  283.6 1.6 copy.48
  285.2 0.7 gather_fusion
  287.2 5.8 %cholesky.33 = f32[64,64]{1,0:T(8,128)S(1)} custom-call(f32[64,64]{1,0:T(8,128)S(1)} %fusion.29), custom_call_target="Cholesky" | custom-call | tf_op jit(solution)/shard_map/jit(cholesky)/cholesky | solution.py:42
  293.1 0.6 compare_reduce_fusion.3
  293.7 0.7 fusion.20
  294.4 4.9 %custom-call.24 = f32[1,64,64]{1,2,0:T(8,128)S(1)} custom-call(f32[1,64,64]{2,1,0:T(8,128)S(1)} %fusion.20), custom_call_target="InvertDiagBlocksLowerTriangular" | custom-call | tf_op jit(solution)/shard_map/triangular_solve/custom-call.3 | solution.py:13
  300.4 1.8 convolution_add_fusion.4
  302.4 0.7 cholesky.94
  303.2 0.6 compare_reduce_fusion.2
  303.8 0.6 fusion.44
  304.5 0.6 custom-call.26
  305.9 0.7 cholesky.105
  306.6 0.6 compare_reduce_fusion.1
  307.3 0.6 fusion.45
  307.9 0.6 custom-call.30
  310.9 0.7 cholesky.116
  311.7 0.6 compare_reduce_fusion
  312.4 0.6 fusion.46
  313.0 0.6 custom-call.32
  314.2 5.2 %convolution_convert_fusion = bf16[8192,8]{0,1:T(8,128)(2,1)} fusion(bf16[512,8192]{1,0:T(8,128)(2,1)} %fusion.1, f32[512,8]{0,1:T(8,128)S(1)} %convolution_add_fusion.1), kind=kOutput, calls=%fused_computation.6 | convolution fusion | flops 67178496 | bytes 8536064 | tf_op jit(solution)/shard_map/rc,rv->cv/dot_general | solution.py:66
  319.5 0.7 constant_dynamic-slice_fusion
  320.1 21.8 %all-gather.4.cloned.1.call-done = bf16[65536,8]{0,1:T(8,128)(2,1)} async-done(((bf16[8192,8]{0,1:T(8,128)(2,1)}), bf16[65536,8]{0,1:T(8,128)(2,1)}) %all-gather.4.cloned.1.call-update) | async-done | bytes 1048592 | tf_op jit(solution)/shard_map/all_gather | solution.py:69
  341.9 2.7 convert_element_type.49
  (60 shorter events, 7.1 us)
Async XLA Ops:
  14.8 5.4 %copy-start.2 = (s32[1,8]{1,0:T(1,128)S(1)}, s32[1,8]{1,0:T(1,128)}, u32[]{:S(2)}) copy-start(s32[1,8]{1,0:T(1,128)} %param.14) | copy-start | bytes 100
  14.8 103.0 %copy-start.1 = (f32[64,8]{0,1:T(8,128)S(1)}, f32[64,8]{0,1:T(8,128)}, u32[]{:S(2)}) copy-start(f32[64,8]{0,1:T(8,128)} %param.13) | copy-start | bytes 6148
  14.8 111.4 %all-to-all-start = ((bf16[64,8,8192]{2,0,1:T(8,128)(2,1)}), bf16[64,8,8192]{2,0,1:T(8,128)(2,1)}, u32[]{:S(2)}, u32[]{:S(2)}) async-start(bf16[64,8,8192]{2,0,1:T(8,128)(2,1)} %bitcast.121), calls=%async_computation | async-start | bytes 16777216 | tf_op jit(solution)/shard_map/all_to_all | solution.py:29
  20.1 263.5 %all-reduce.2.cloned.1.call-start = ((), (), s32[]{:S(2)}) async-start(), calls=%async_computation.1 | async-start | bytes 2097152 | tf_op jit(solution)/shard_map/psum | solution.py:33
  151.8 190.1 %all-gather.4.cloned.1.call-start = ((), (), s32[]{:S(2)}) async-start(), calls=%async_computation.2 | async-start | bytes 1179648 | tf_op jit(solution)/shard_map/all_gather | solution.py:69
  283.6 26.5 %copy-start = (f32[512,512]{1,0:T(8,128)S(1)}, f32[512,512]{1,0:T(8,128)}, u32[]{:S(2)}) copy-start(f32[512,512]{1,0:T(8,128)} %all-reduce.2.cloned.1.call-done) | copy-start | bytes 3145732
Sparse Core Ops, SparseCore 0:
  151.9 131.6 all-reduce.1
  319.6 22.3 all-gather.3
where the time goes:
time: 352 us; the launch traced here: 351 us
  waiting for transfers between devices  145 us (41%)
  blocking collectives  106 us (30%)
  other arithmetic  46.2 us (13%)
  matrix products  23.4 us (7%)
  between operations  14.2 us (4%)
  local copies, waits for them, and re-layouts  11.8 us (3%)
  starting transfers between devices  5.59 us (2%)
    psum x1, waiting for transfers between devices, gram_body(): lax.psum(jnp.einsum('rc,kc->rk', centered, centered, preferred_element_ty...  123 us
    all_gather x1, blocking collectives, gram_body(): all_picks = lax.all_gather(nys_rows, 'samp', axis=0, tiled=True)  97.4 us
    all_gather x1, waiting for transfers between devices, gram_body(): lax.all_gather(local_update.astype(jnp.bfloat16), 'samp', axis=0, tiled=T...  21.8 us
    dot_general x1, matrix products, gram_body(): jnp.einsum('rc,kc->rk', centered, centered, preferred_element_type=jnp.fl...  11.3 us
    another operation x8, other arithmetic, factor_solve(): lax.linalg.triangular_solve(factor, middle, left_side=True, lower=True, t...  9.37 us
    another operation x1, other arithmetic  8.89 us
    convert_element_type x1, other arithmetic, gram_body(): ((widened - col_mean) * (1.0 / math.sqrt(total_cols))).astype(jnp.bfloat16)  8.89 us
    all_gather x1, blocking collectives, gram_body(): all_energies = lax.all_gather(energies, 'samp', axis=0, tiled=True)  8.27 us
  transfers between devices with their start and end apart: 3, of which 2 were waited for; matrix products, arithmetic and copies ran while one was open for 3% of the time, Pallas kernels for 0%

commit v1 on v0

--- a/solution.py
+++ b/solution.py
@@ -35,7 +35,14 @@
         ("samp", "par"),
     )
     all_energies = lax.all_gather(energies, "samp", axis=0, tiled=True)
-    all_picks = lax.all_gather(nys_rows, "samp", axis=0, tiled=True)
+    size = lax.axis_size("samp")
+    hops = [(i, (i + 1) % size) for i in range(size)]
+    terms = [nys_rows]
+    for stride in range(1, size):
+        terms = [lax.ppermute(terms[0], "samp", hops), *terms]
+    whole = jnp.concatenate(terms, axis=0)
+    shift = (lax.axis_index("samp") + 1) * terms[-1].shape[0]
+    all_picks = jnp.roll(whole, shift, axis=0)
     selected = (jnp.arange(groups, dtype=jnp.int32)[:, None] * samp_rows + all_picks).reshape(-1)
     sketch = jnp.take(gram, selected, axis=1)
     core_block = jnp.take(sketch, selected, axis=0)

time: 352 us -> 367 us (1.043)
  waiting for transfers between devices: 145 us -> 167 us
  blocking collectives: 106 us -> 97.1 us
    all_gather x1 -> x0, blocking collectives: 97.4 us -> none  [gram_body(): all_picks = lax.all_gather(nys_rows, 'samp', axis=0, tiled=True)]
    all_gather x1, blocking collectives: 8.27 us -> 97.1 us  [gram_body(): all_energies = lax.all_gather(energies, 'samp', axis=0, tiled=True)]
    ppermute x0 -> x7, waiting for transfers between devices: none -> 23 us  [gram_body(): terms = [lax.ppermute(terms[0], 'samp', hops), *terms]]
  transfers between devices with their start and end apart: 3 -> 10, of which waited for: 2 -> 8; matrix products, arithmetic and copies ran while one was open for 3% -> 3% of each run, Pallas kernels for 0% -> 0%
where the time goes in v1:
time: 367 us; the launch traced here: 366 us
  waiting for transfers between devices  167 us (46%)
  blocking collectives  97.1 us (26%)
  other arithmetic  46.2 us (13%)
  matrix products  23.4 us (6%)
  between operations  14.2 us (4%)
  local copies, waits for them, and re-layouts  11.9 us (3%)
  starting transfers between devices  6.48 us (2%)
    psum x1, waiting for transfers between devices, gram_body(): lax.psum(jnp.einsum('rc,kc->rk', centered, centered, preferred_element_ty...  122 us
    all_gather x1, blocking collectives, gram_body(): all_energies = lax.all_gather(energies, 'samp', axis=0, tiled=True)  97.1 us
    ppermute x7, waiting for transfers between devices, gram_body(): terms = [lax.ppermute(terms[0], 'samp', hops), *terms]  23 us
    all_gather x1, waiting for transfers between devices, gram_body(): lax.all_gather(local_update.astype(jnp.bfloat16), 'samp', axis=0, tiled=T...  21.8 us
    dot_general x1, matrix products, gram_body(): jnp.einsum('rc,kc->rk', centered, centered, preferred_element_type=jnp.fl...  11.3 us
    another operation x8, other arithmetic, factor_solve(): lax.linalg.triangular_solve(factor, middle, left_side=True, lower=True, t...  9.37 us
    another operation x1, other arithmetic  8.89 us
    convert_element_type x1, other arithmetic, gram_body(): ((widened - col_mean) * (1.0 / math.sqrt(total_cols))).astype(jnp.bfloat16)  8.89 us
  transfers between devices with their start and end apart: 10, of which 8 were waited for; matrix products, arithmetic and copies ran while one was open for 3% of the time, Pallas kernels for 0%

profile of v1, /device:TPU:0, one launch (start us, length us, event | category | flops | bytes accessed | tf_op | source)
XLA Modules:
  0.0 366.1 jit_solution(11186264684654968957)
XLA Ops:
  7.2 7.6 %copy.62 = bf16[8,8,8,8192]{3,2,0,1:T(8,128)(2,1)} copy(bf16[8,8,8,8192]{3,2,1,0:T(8,128)(2,1)} %bitcast.120) | data formatting | bytes 16777216 | tf_op jit(solution)/shard_map/all_to_all | solution.py:29
  14.8 5.3 %all-to-all-start = ((bf16[64,8,8192]{2,0,1:T(8,128)(2,1)}), bf16[64,8,8192]{2,0,1:T(8,128)(2,1)}, u32[]{:S(2)}, u32[]{:S(2)}) async-start(bf16[64,8,8192]{2,0,1:T(8,128)(2,1)} %bitcast.119), calls=%async_computation | async-start | bytes 16777216 | tf_op jit(solution)/shard_map/all_to_all | solution.py:29
  20.7 97.1 %all-gather = f32[8,64,8]{1,2,0:T(8,128)S(1)} all-gather(f32[1,64,8]{1,2,0:T(8,128)S(1)} %bitcast.122), channel_id=1, replica_groups=mesh['samp'=8,'par'=4] {'samp'}, dimensions={0}, use_global_device_ids=true | all-gather | bytes 18432 | tf_op jit(solution)/shard_map/all_gather | solution.py:37
  118.2 3.5 collective-permute-done.1
  121.8 3.9 %collective-permute-done.2 = s32[1,8]{1,0:T(1,128)S(1)} collective-permute-done((s32[1,8]{1,0:T(1,128)S(1)}, s32[1,8]{1,0:T(1,128)S(1)}, u32[]{:S(2)}, u32[]{:S(2)}) %collective-permute-start.2) | collective-permute-done | bytes 64 | tf_op jit(solution)/shard_map/ppermute | solution.py:42
  125.7 3.9 %collective-permute-done.3 = s32[1,8]{1,0:T(1,128)S(1)} collective-permute-done((s32[1,8]{1,0:T(1,128)S(1)}, s32[1,8]{1,0:T(1,128)S(1)}, u32[]{:S(2)}, u32[]{:S(2)}) %collective-permute-start.3) | collective-permute-done | bytes 64 | tf_op jit(solution)/shard_map/ppermute | solution.py:42
  129.6 3.9 %collective-permute-done.4 = s32[1,8]{1,0:T(1,128)S(1)} collective-permute-done((s32[1,8]{1,0:T(1,128)S(1)}, s32[1,8]{1,0:T(1,128)S(1)}, u32[]{:S(2)}, u32[]{:S(2)}) %collective-permute-start.4) | collective-permute-done | bytes 64 | tf_op jit(solution)/shard_map/ppermute | solution.py:42
  133.4 3.9 %collective-permute-done.5 = s32[1,8]{1,0:T(1,128)S(1)} collective-permute-done((s32[1,8]{1,0:T(1,128)S(1)}, s32[1,8]{1,0:T(1,128)S(1)}, u32[]{:S(2)}, u32[]{:S(2)}) %collective-permute-start.5) | collective-permute-done | bytes 64 | tf_op jit(solution)/shard_map/ppermute | solution.py:42
  137.3 3.9 %collective-permute-done.6 = s32[1,8]{1,0:T(1,128)S(1)} collective-permute-done((s32[1,8]{1,0:T(1,128)S(1)}, s32[1,8]{1,0:T(1,128)S(1)}, u32[]{:S(2)}, u32[]{:S(2)}) %collective-permute-start.6) | collective-permute-done | bytes 64 | tf_op jit(solution)/shard_map/ppermute | solution.py:42
  141.6 5.5 %convert_reduce_fusion = f32[8192]{0:T(1024)S(1)} fusion(bf16[64,8,8192]{2,0,1:T(8,128)(2,1)} %all-to-all-done), kind=kLoop, calls=%fused_computation.8 | loop fusion | flops 8380416 | bytes 8421376 | tf_op jit(solution)/shard_map/reduce_sum | solution.py:31
  147.0 8.9 %multiply_convert_fusion = bf16[64,8,8192]{2,0,1:T(8,128)(2,1)} fusion(bf16[64,8,8192]{2,0,1:T(8,128)(2,1)} %all-to-all-done, f32[8192]{0:T(1024)S(1)} %broadcast_multiply_fusion), kind=kLoop, calls=%fused_computation.5 | loop fusion | flops 16777216 | bytes 16809984 | tf_op jit(solution)/shard_map/convert.2
  155.9 11.3 %fusion.73 = f32[512,512]{1,0:T(8,128)} fusion(bf16[512,8192]{1,0:T(8,128)(2,1)} %bitcast.121), kind=kOutput, calls=%fused_computation.118 | convolution fusion | flops 4294967296 | bytes 9437184 | tf_op jit(solution)/shard_map/rc,kc->rk/dot_general | solution.py:34
  167.4 8.9 %fusion.1 = bf16[512,8192]{1,0:T(8,128)(2,1)} fusion(bf16[64,8,8192]{2,0,1:T(8,128)(2,1)} %all-to-all-done, f32[8192]{0:T(1024)S(1)} %broadcast_multiply_fusion), kind=kLoop, calls=%fused_computation.4 | loop fusion | flops 16777216 | bytes 16809984 | tf_op jit(solution)/shard_map/convert_element_type | solution.py:32
  176.3 121.9 %all-reduce.2.cloned.1.call-done = f32[512,512]{1,0:T(8,128)} async-done(((f32[512,512]{1,0:T(8,128)}), f32[512,512]{1,0:T(8,128)}) %all-reduce.2.cloned.1.call-update) | async-done | bytes 1048592 | tf_op jit(solution)/shard_map/psum | solution.py:33
  298.2 1.6 copy.48
  299.9 0.7 gather_fusion
  301.8 5.8 %cholesky.33 = f32[64,64]{1,0:T(8,128)S(1)} custom-call(f32[64,64]{1,0:T(8,128)S(1)} %fusion.29), custom_call_target="Cholesky" | custom-call | tf_op jit(solution)/shard_map/jit(cholesky)/cholesky | solution.py:49
  308.3 0.7 fusion.20
  309.0 4.9 %custom-call.24 = f32[1,64,64]{1,2,0:T(8,128)S(1)} custom-call(f32[1,64,64]{2,1,0:T(8,128)S(1)} %fusion.20), custom_call_target="InvertDiagBlocksLowerTriangular" | custom-call | tf_op jit(solution)/shard_map/triangular_solve/custom-call.3 | solution.py:13
  315.0 1.8 convolution_add_fusion.4
  317.1 0.7 cholesky.94
  317.8 0.6 compare_reduce_fusion.2
  318.5 0.6 fusion.44
  320.5 0.7 cholesky.105
  321.3 0.6 compare_reduce_fusion.1
  321.9 0.6 fusion.45
  325.6 0.7 cholesky.116
  327.0 0.6 fusion.46
  328.8 5.2 %convolution_convert_fusion = bf16[8192,8]{0,1:T(8,128)(2,1)} fusion(bf16[512,8192]{1,0:T(8,128)(2,1)} %fusion.1, f32[512,8]{0,1:T(8,128)S(1)} %convolution_add_fusion.1), kind=kOutput, calls=%fused_computation.6 | convolution fusion | flops 67178496 | bytes 8536064 | tf_op jit(solution)/shard_map/rc,rv->cv/dot_general | solution.py:73
  334.1 0.7 constant_dynamic-slice_fusion
  334.8 21.8 %all-gather.3.cloned.1.call-done = bf16[65536,8]{0,1:T(8,128)(2,1)} async-done(((bf16[8192,8]{0,1:T(8,128)(2,1)}), bf16[65536,8]{0,1:T(8,128)(2,1)}) %all-gather.3.cloned.1.call-update) | async-done | bytes 1048592 | tf_op jit(solution)/shard_map/all_gather | solution.py:76
  356.6 2.7 convert_element_type.49
  (74 shorter events, 11.2 us)
Async XLA Ops:
  14.8 5.4 %copy-start.2 = (s32[1,8]{1,0:T(1,128)S(1)}, s32[1,8]{1,0:T(1,128)}, u32[]{:S(2)}) copy-start(s32[1,8]{1,0:T(1,128)} %param.14) | copy-start | bytes 100
  14.8 5.9 %copy-start.1 = (f32[64,8]{0,1:T(8,128)S(1)}, f32[64,8]{0,1:T(8,128)}, u32[]{:S(2)}) copy-start(f32[64,8]{0,1:T(8,128)} %param.13) | copy-start | bytes 6148
  14.8 126.8 %all-to-all-start = ((bf16[64,8,8192]{2,0,1:T(8,128)(2,1)}), bf16[64,8,8192]{2,0,1:T(8,128)(2,1)}, u32[]{:S(2)}, u32[]{:S(2)}) async-start(bf16[64,8,8192]{2,0,1:T(8,128)(2,1)} %bitcast.119), calls=%async_computation | async-start | bytes 16777216 | tf_op jit(solution)/shard_map/all_to_all | solution.py:29
  20.1 278.2 %all-reduce.2.cloned.1.call-start = ((), (), s32[]{:S(2)}) async-start(), calls=%async_computation.1 | async-start | bytes 2097152 | tf_op jit(solution)/shard_map/psum | solution.py:33
  20.1 97.7 %collective-permute-start = (s32[1,8]{1,0:T(1,128)S(1)}, s32[1,8]{1,0:T(1,128)S(1)}, u32[]{:S(2)}, u32[]{:S(2)}) collective-permute-start(s32[1,8]{1,0:T(1,128)S(1)} %copy-done.2), channel_id=1, source_target_pairs={{0,4},{4,8},{8,12},{12,16},{16,20},{20,24},{24,28},{28,0},{1,5},{5... | collective-permute-start | bytes 104 | tf_op jit(solution)/shard_map/ppermute | solution.py:42
  117.8 3.9 %collective-permute-start.1 = (s32[1,8]{1,0:T(1,128)S(1)}, s32[1,8]{1,0:T(1,128)S(1)}, u32[]{:S(2)}, u32[]{:S(2)}) collective-permute-start(s32[1,8]{1,0:T(1,128)S(1)} %collective-permute-done), channel_id=1, source_target_pairs={{0,4},{4,8},{8,12},{12,16},{16,20},{20,24},{24,28},{28,0},{1,5},{5... | collective-permute-start | bytes 104 | tf_op jit(solution)/shard_map/ppermute | solution.py:42
  121.8 3.9 %collective-permute-start.2 = (s32[1,8]{1,0:T(1,128)S(1)}, s32[1,8]{1,0:T(1,128)S(1)}, u32[]{:S(2)}, u32[]{:S(2)}) collective-permute-start(s32[1,8]{1,0:T(1,128)S(1)} %collective-permute-done.1), channel_id=1, source_target_pairs={{0,4},{4,8},{8,12},{12,16},{16,20},{20,24},{24,28},{28,0},{1,5},{5... | collective-permute-start | bytes 104 | tf_op jit(solution)/shard_map/ppermute | solution.py:42
  125.7 3.9 %collective-permute-start.3 = (s32[1,8]{1,0:T(1,128)S(1)}, s32[1,8]{1,0:T(1,128)S(1)}, u32[]{:S(2)}, u32[]{:S(2)}) collective-permute-start(s32[1,8]{1,0:T(1,128)S(1)} %collective-permute-done.2), channel_id=1, source_target_pairs={{0,4},{4,8},{8,12},{12,16},{16,20},{20,24},{24,28},{28,0},{1,5},{5... | collective-permute-start | bytes 104 | tf_op jit(solution)/shard_map/ppermute | solution.py:42
  129.5 3.9 %collective-permute-start.4 = (s32[1,8]{1,0:T(1,128)S(1)}, s32[1,8]{1,0:T(1,128)S(1)}, u32[]{:S(2)}, u32[]{:S(2)}) collective-permute-start(s32[1,8]{1,0:T(1,128)S(1)} %collective-permute-done.3), channel_id=1, source_target_pairs={{0,4},{4,8},{8,12},{12,16},{16,20},{20,24},{24,28},{28,0},{1,5},{5... | collective-permute-start | bytes 104 | tf_op jit(solution)/shard_map/ppermute | solution.py:42
  133.4 3.9 %collective-permute-start.5 = (s32[1,8]{1,0:T(1,128)S(1)}, s32[1,8]{1,0:T(1,128)S(1)}, u32[]{:S(2)}, u32[]{:S(2)}) collective-permute-start(s32[1,8]{1,0:T(1,128)S(1)} %collective-permute-done.4), channel_id=1, source_target_pairs={{0,4},{4,8},{8,12},{12,16},{16,20},{20,24},{24,28},{28,0},{1,5},{5... | collective-permute-start | bytes 104 | tf_op jit(solution)/shard_map/ppermute | solution.py:42
  137.3 3.9 %collective-permute-start.6 = (s32[1,8]{1,0:T(1,128)S(1)}, s32[1,8]{1,0:T(1,128)S(1)}, u32[]{:S(2)}, u32[]{:S(2)}) collective-permute-start(s32[1,8]{1,0:T(1,128)S(1)} %collective-permute-done.5), channel_id=1, source_target_pairs={{0,4},{4,8},{8,12},{12,16},{16,20},{20,24},{24,28},{28,0},{1,5},{5... | collective-permute-start | bytes 104 | tf_op jit(solution)/shard_map/ppermute | solution.py:42
  167.2 189.4 %all-gather.3.cloned.1.call-start = ((), (), s32[]{:S(2)}) async-start(), calls=%async_computation.2 | async-start | bytes 1179648 | tf_op jit(solution)/shard_map/all_gather | solution.py:76
  298.2 26.5 %copy-start = (f32[512,512]{1,0:T(8,128)S(1)}, f32[512,512]{1,0:T(8,128)}, u32[]{:S(2)}) copy-start(f32[512,512]{1,0:T(8,128)} %all-reduce.2.cloned.1.call-done) | copy-start | bytes 3145732
Sparse Core Ops, SparseCore 0:
  167.3 130.8 all-reduce.1
  334.2 22.3 all-gather.2
